TPU v7x, 128 devices: a whole 4x4x4 slice. The times are simulated.
128 devices in a mesh: dp: 32 (over x, y, core), mp: 4 (over z).
Axes of the slice: x: 4, y: 4, z: 4, core: 2. Of those that a mesh axis runs over, the one named last changes fastest.
Arguments:
- grad_parts: bfloat16 [32, 4, 1024, 4096], P('dp', None, None, 'mp'), may hold values from -4000 to 4000
- master: float32 [4, 1024, 4096], P(None, 'dp', 'mp'), may hold values from -6 to 6
- first_moment: float32 [4, 1024, 4096], P(None, 'dp', 'mp'), may hold values from -4 to 4
- second_moment: float32 [4, 1024, 4096], P(None, 'dp', 'mp'), may hold values from 0.25 to 4
- left_basis: bfloat16 [4, 1024, 4096], P(None, 'dp', 'mp'), may hold values from -1 to 1, as said below
- right_basis: bfloat16 [4, 1024, 4096], P(None, 'dp', 'mp'), may hold values from -1 to 1, as said below
Outputs:
- weights: bfloat16 [4, 1024, 4096], P(None, None, 'mp')
- new_master: float32 [4, 1024, 4096], P(None, 'dp', 'mp')
- new_first: float32 [4, 1024, 4096], P(None, 'dp', 'mp')
- new_second: float32 [4, 1024, 4096], P(None, 'dp', 'mp')
Inputs may be any that keep to these rules, and one draw needn't show every extreme that they name: Each block left_basis[i, :, j * 1024 : (j + 1) * 1024] is an orthogonal 1024 x 1024 matrix up to rounding. Each block right_basis[i, :, j * 1024 : (j + 1) * 1024] is an orthogonal 1024 x 1024 matrix up to rounding.
All inputs are finite; a program needn't handle non-finite values.
Results may differ from a plain program's by a relative error of at most 0.02.
Values may be sent and summed in bfloat16 or wider, within the bound.
No kernel may reach another device: no remote copies, remote signals or barrier semaphores. Data moves between devices by JAX's collectives and lax.ppermute only.
A program may use at most 128 MiB of HBM per device.

v0:
```python
import jax
import jax.numpy as jnp
from jax import lax
from jax.sharding import Mesh
from jax.sharding import PartitionSpec as P

D = 4096
STEP = 10
DP = ("dp_0", "dp_1", "dp_2")
DP_MP = ("dp_0", "dp_1", "dp_2", "mp")


beta_one = 0.95
beta_two = 0.95
epsilon = 1e-08
norm_epsilon = 1e-06
learning_rate = 0.3
decay_rate = 0.1


def over_axes(array, axes):
    for axis in axes:
        array = lax.psum(array, axis)
    return array


def split_up(array, dim, peers):
    before, after = (array.shape[:dim], array.shape[dim + 1 :])
    return jnp.moveaxis(array.reshape(*before, peers, -1, *after), dim, 0)


def summed_rows(array, chips, core, dim):
    sizes = (lax.axis_size(chips), lax.axis_size(core))
    parts = split_up(array, dim, sizes[0] * sizes[1])
    inside = parts.shape[1:]
    parts = parts.reshape(*sizes, *inside).swapaxes(0, 1).reshape(-1, *inside)
    parts = lax.psum_scatter(parts, core, scatter_dimension=0, tiled=True)
    return lax.psum_scatter(parts, chips, scatter_dimension=0, tiled=True)[0]


def per_device(grad_parts, master, first_moment, second_moment, left_basis, right_basis):
    gradient = lax.psum_scatter(grad_parts[0], DP, scatter_dimension=1, tiled=True).astype(
        jnp.float32
    )
    squares_sum = over_axes(jnp.sum(gradient * gradient), DP_MP)
    clip_scale = jnp.minimum(1.0, 2.0 * D / jnp.sqrt(squares_sum + norm_epsilon))
    grad_low = gradient.astype(jnp.bfloat16)
    right_full = lax.all_gather(right_basis, DP, axis=1, tiled=True)
    turned = jnp.einsum(
        "isk,ikb->isb", grad_low, right_full, preferred_element_type=jnp.float32
    ).astype(jnp.bfloat16)
    left_cols = left_basis
    raw_term = jnp.einsum("isx,isb->xib", left_cols, turned, preferred_element_type=jnp.float32)
    rotated_rows = summed_rows(
        lax.optimization_barrier(raw_term.astype(jnp.bfloat16))
        .astype(jnp.float32)
        .astype(jnp.bfloat16),
        ("dp_0", "dp_1"),
        "dp_2",
        0,
    ).astype(jnp.float32)
    rotated = jnp.transpose(rotated_rows, (1, 0, 2))
    clipped = clip_scale * rotated
    new_first = beta_one * first_moment + (1.0 - beta_one) * clipped
    new_second = beta_two * second_moment + (1.0 - beta_two) * clipped * clipped
    bias_one = 1.0 - beta_one**STEP
    bias_two = 1.0 - beta_two**STEP
    direction = (new_first / bias_one / (jnp.sqrt(new_second / bias_two) + epsilon)).astype(
        jnp.bfloat16
    )
    back_rows = jnp.einsum(
        "isb,icb->isc", direction, right_full, preferred_element_type=jnp.float32
    ).astype(jnp.bfloat16)
    left_cols = left_basis
    update = jnp.einsum(
        "isk,ikc->isc",
        left_cols,
        lax.all_gather(back_rows, DP, axis=1, tiled=True),
        preferred_element_type=jnp.float32,
    )
    new_master = master * (1.0 - learning_rate * decay_rate) - learning_rate * update
    weights = lax.all_gather(new_master.astype(jnp.bfloat16), DP, axis=1, tiled=True)
    return (weights, new_master, new_first, new_second)


def solution(mesh):
    finer = Mesh(mesh.devices.reshape(4, 4, 2, mesh.shape["mp"]), ("dp_0", "dp_1", "dp_2", "mp"))
    placed = (
        P(DP, None, None, "mp"),
        P(None, DP, "mp"),
        P(None, DP, "mp"),
        P(None, DP, "mp"),
        P(None, DP, "mp"),
        P(None, DP, "mp"),
    )
    return jax.shard_map(
        per_device,
        mesh=finer,
        in_specs=placed,
        out_specs=(P(None, None, "mp"), P(None, DP, "mp"), P(None, DP, "mp"), P(None, DP, "mp")),
        check_vma=False,
    )
```

profile of v0, /device:TPU:1, one launch (start us, length us, event | category | flops | bytes accessed | tf_op | source)
XLA Modules:
  0.0 428.3 jit_solution(16834403755977702970)
XLA Ops:
  7.2 0.7 reduce-scatter.6.cloned.1.call-update
  8.0 0.7 all-gather.4.cloned.1.call-update
  8.7 0.0 reduce-scatter.8.cloned.1.call-start
  8.7 97.1 %reduce-scatter.6.cloned.1.call-done = bf16[4,32,1024]{2,1,0:T(8,128)(2,1)} async-done(((bf16[4,1024,1024]{2,1,0:T(8,128)(2,1)}), bf16[4,32,1024]{2,1,0:T(8,128)(2,1)}) %reduce-scatter.6.cloned.1.call-update) | async-done | bytes 262160 | tf_op jit(solution)/shard_map/reduce_scatter | solution.py:42
  105.8 56.5 %all-gather.4.cloned.1.call-done = bf16[4,1024,1024]{2,1,0:T(8,128)(2,1)} async-done(((bf16[4,32,1024]{2,1,0:T(8,128)(2,1)}), bf16[4,1024,1024]{2,1,0:T(8,128)(2,1)}) %all-gather.4.cloned.1.call-update) | async-done | bytes 8388624 | tf_op jit(solution)/shard_map/all_gather | solution.py:48
  162.3 10.8 %convert_bitcast_fusion = bf16[1024,4,1024]{0,2,1:T(8,128)(2,1)} fusion(bf16[4,32,1024]{2,1,0:T(8,128)(2,1)S(1)} %copy-done, bf16[4,32,1024]{2,1,0:T(8,128)(2,1)} %reduce-scatter.6.cloned.1.call-done, bf16[4,1024,1024]{2,1,0:T(8,128)(2,1)} %all-gather.4.cloned.1.call-done), kind=kOutput, calls=%fused_computation | convolution fusion | flops 541196288 | bytes 17301504 | tf_op jit(solution)/shard_map/isx,isb->xib/dot_general | solution.py:53
  173.2 11.4 %copy.14 = bf16[1024,4,1024]{2,0,1:T(8,128)(2,1)} copy(bf16[1024,4,1024]{0,2,1:T(8,128)(2,1)} %convert_bitcast_fusion) | data formatting | bytes 16777216 | tf_op jit(solution)/shard_map/optimization_barrier | solution.py:55
  184.6 8.6 %copy.15 = bf16[2,16,32,4,1024]{4,2,3,1,0:T(8,128)(2,1)} copy(bf16[2,16,32,4,1024]{4,2,0,1,3:T(8,128)(2,1)} %bitcast.24) | data formatting | bytes 16777216 | tf_op jit(solution)/shard_map/transpose | solution.py:36
  193.3 0.0 reduce-scatter.10.cloned.1.call-start
  193.3 18.8 %reduce-scatter.8.cloned.1.call-done = bf16[16,32,4,1024]{3,1,2,0:T(8,128)(2,1)} async-done(((bf16[32,32,4,1024]{3,1,2,0:T(8,128)(2,1)}), bf16[16,32,4,1024]{3,1,2,0:T(8,128)(2,1)}) %reduce-scatter.8.cloned.1.call-update) | async-done | bytes 4194320 | tf_op jit(solution)/shard_map/reduce_scatter | solution.py:37
  212.1 0.0 all-gather.6.cloned.1.call-start
  212.2 0.7 multiply_reduce_fusion
  212.9 9.1 %psum.28 = f32[]{:T(128)} all-reduce(f32[]{:T(128)} %multiply_reduce_fusion), channel_id=1, replica_groups=mesh['dp_0'=4,'dp_1'=4,'dp_2'=2,'mp'=4] {'dp_0'}, use_global_device_ids=true, to_apply=%region_2.0 | all-reduce | flops 1 | bytes 8 | tf_op jit(solution)/shard_map/psum | solution.py:23
  222.0 9.5 %psum.29 = f32[]{:T(128)} all-reduce(f32[]{:T(128)} %psum.28), channel_id=1, replica_groups=mesh['dp_0'=4,'dp_1'=4,'dp_2'=2,'mp'=4] {'dp_1'}, use_global_device_ids=true, to_apply=%region_3.0 | all-reduce | flops 1 | bytes 8 | tf_op jit(solution)/shard_map/psum | solution.py:23
  231.5 6.7 %psum.30 = f32[]{:T(128)} all-reduce(f32[]{:T(128)} %psum.29), channel_id=1, replica_groups=mesh['dp_0'=4,'dp_1'=4,'dp_2'=2,'mp'=4] {'dp_2'}, use_global_device_ids=true, to_apply=%region_4.0 | all-reduce | flops 1 | bytes 8 | tf_op jit(solution)/shard_map/psum | solution.py:23
  238.2 9.5 %psum.31 = f32[]{:T(128)} all-reduce(f32[]{:T(128)} %psum.30), channel_id=1, replica_groups=mesh['dp_0'=4,'dp_1'=4,'dp_2'=2,'mp'=4] {'mp'}, use_global_device_ids=true, to_apply=%region_5.0 | all-reduce | flops 1 | bytes 8 | tf_op jit(solution)/shard_map/psum | solution.py:23
  248.4 44.5 %reduce-scatter.10.cloned.1.call-done = bf16[1,32,4,1024]{3,1,2,0:T(8,128)(2,1)} async-done(((bf16[16,32,4,1024]{3,1,2,0:T(8,128)(2,1)}), bf16[1,32,4,1024]{3,1,2,0:T(8,128)(2,1)}) %reduce-scatter.10.cloned.1.call-update) | async-done | bytes 262160
  293.0 1.1 multiply_add_fusion
  294.1 7.0 %convolution_convert_fusion = bf16[4,32,1024]{2,1,0:T(8,128)(2,1)} fusion(bf16[4,1024,1024]{2,1,0:T(8,128)(2,1)} %all-gather.4.cloned.1.call-done, f32[4,32,1024]{2,1,0:T(8,128)S(1)} %get-tuple-element.15, f32[4,32,1024]{2,1,0:T(8,128)S(1)} %get-tuple-element.14), kind=kOutput, calls=%fused_computation.4 | convolution fusion | flops 269221888 | bytes 9699328 | tf_op jit(solution)/shard_map/isb,icb->isc/dot_general | solution.py:71
  301.2 0.0 all-gather.8.cloned.1.call-start
  301.2 54.2 %all-gather.6.cloned.1.call-done = bf16[4,1024,1024]{2,1,0:T(8,128)(2,1)} async-done(((bf16[4,32,1024]{2,1,0:T(8,128)(2,1)}), bf16[4,1024,1024]{2,1,0:T(8,128)(2,1)}) %all-gather.6.cloned.1.call-update) | async-done | bytes 8388624 | tf_op jit(solution)/shard_map/all_gather | solution.py:78
  355.4 5.8 %fusion.7 = (bf16[4,32,1024]{2,1,0:T(8,128)(2,1)}, f32[4,32,1024]{2,1,0:T(8,128)}) fusion(bf16[4,32,1024]{2,1,0:T(8,128)(2,1)S(1)} %copy-done, bf16[4,1024,1024]{2,1,0:T(8,128)(2,1)} %all-gather.6.cloned.1.call-done, f32[4,32,1024]{2,1,0:T(8,128)S(1)} %copy-done.6), kind=kOutput, calls=%fused_computation.16 | convolution fusion | flops 268959744 | bytes 9961472 | tf_op jit(solution)/shard_map/isk,ikc->isc/dot_general | solution.py:75
  361.3 52.4 %all-gather.8.cloned.1.call-done = bf16[4,1024,1024]{2,1,0:T(8,128)(2,1)} async-done(((bf16[4,32,1024]{2,1,0:T(8,128)(2,1)}), bf16[4,1024,1024]{2,1,0:T(8,128)(2,1)}) %all-gather.8.cloned.1.call-update) | async-done | bytes 8388624 | tf_op jit(solution)/shard_map/all_gather | solution.py:82
  413.7 7.8 %copy.17 = bf16[4,1024,1024]{2,1,0:T(8,128)(2,1)} copy(bf16[4,1024,1024]{2,1,0:T(8,128)(2,1)} %all-gather.8.cloned.1.call-done) | data formatting | bytes 16777216
  (20 shorter events, 0.2 us)
Async XLA Ops:
  7.2 155.2 %copy-start = (bf16[4,32,1024]{2,1,0:T(8,128)(2,1)S(1)}, bf16[4,32,1024]{2,1,0:T(8,128)(2,1)}, u32[]{:S(2)}) copy-start(bf16[4,32,1024]{2,1,0:T(8,128)(2,1)} %param.10) | copy-start | bytes 786436
  7.2 98.6 %reduce-scatter.6.cloned.1.call-start = ((), (), s32[]{:S(2)}) async-start(), calls=%async_computation.3 | async-start | bytes 8650752 | tf_op jit(solution)/shard_map/reduce_scatter | solution.py:42
  7.9 154.4 %all-gather.4.cloned.1.call-start = ((), (), s32[]{:S(2)}) async-start(), calls=%async_computation.4 | async-start | bytes 8650752 | tf_op jit(solution)/shard_map/all_gather | solution.py:48
  8.7 203.4 %reduce-scatter.8.cloned.1.call-start = ((), (), s32[]{:S(2)}) async-start(), calls=%async_computation.5 | async-start | bytes 12582912 | tf_op jit(solution)/shard_map/reduce_scatter | solution.py:37
  193.2 19.0 %copy-start.3 = (bf16[4,32,1024]{2,1,0:T(8,128)(2,1)S(1)}, bf16[4,32,1024]{2,1,0:T(8,128)(2,1)}, u32[]{:S(2)}) copy-start(bf16[4,32,1024]{2,1,0:T(8,128)(2,1)} %reduce-scatter.6.cloned.1.call-done) | copy-start | bytes 786436
  193.2 99.7 %copy-start.4 = (f32[4,32,1024]{2,1,0:T(8,128)S(1)}, f32[4,32,1024]{2,1,0:T(8,128)}, u32[]{:S(2)}) copy-start(f32[4,32,1024]{2,1,0:T(8,128)} %param.8) | copy-start | bytes 1572868
  193.2 99.7 %copy-start.5 = (f32[4,32,1024]{2,1,0:T(8,128)S(1)}, f32[4,32,1024]{2,1,0:T(8,128)}, u32[]{:S(2)}) copy-start(f32[4,32,1024]{2,1,0:T(8,128)} %param.9) | copy-start | bytes 1572868
  193.3 99.7 %reduce-scatter.10.cloned.1.call-start = ((), (), s32[]{:S(2)}) async-start(), calls=%async_computation.8 | async-start | bytes 4456448
  212.1 143.3 %copy-start.6 = (f32[4,32,1024]{2,1,0:T(8,128)S(1)}, f32[4,32,1024]{2,1,0:T(8,128)}, u32[]{:S(2)}) copy-start(f32[4,32,1024]{2,1,0:T(8,128)} %param.7) | copy-start | bytes 1572868
  212.1 143.3 %all-gather.6.cloned.1.call-start = ((), (), s32[]{:S(2)}) async-start(), calls=%async_computation.6 | async-start | bytes 8650752 | tf_op jit(solution)/shard_map/all_gather | solution.py:78
  294.1 67.1 %copy-start.1 = (f32[4,32,1024]{2,1,0:T(8,128)}, f32[4,32,1024]{2,1,0:T(8,128)S(1)}, u32[]{:S(2)}) copy-start(f32[4,32,1024]{2,1,0:T(8,128)S(1)} %get-tuple-element.14) | copy-start | bytes 1572868
  294.1 67.1 %copy-start.2 = (f32[4,32,1024]{2,1,0:T(8,128)}, f32[4,32,1024]{2,1,0:T(8,128)S(1)}, u32[]{:S(2)}) copy-start(f32[4,32,1024]{2,1,0:T(8,128)S(1)} %get-tuple-element.15) | copy-start | bytes 1572868
  301.2 112.5 %all-gather.8.cloned.1.call-start = ((), (), s32[]{:S(2)}) async-start(), calls=%async_computation.7 | async-start | bytes 8650752 | tf_op jit(solution)/shard_map/all_gather | solution.py:82
Sparse Core Ops, SparseCore 0:
  11.7 94.0 reduce-scatter.5
  108.2 54.1 all-gather.3
  193.4 18.6 reduce-scatter.7
  215.3 77.5 reduce-scatter.9
  301.3 54.0 all-gather.5
  361.4 52.2 all-gather.7
where the time goes:
time: 429 us; the launch traced here: 428 us
  waiting for transfers between devices  325 us (76%)
  blocking collectives  34.8 us (8%)
  local copies, waits for them, and re-layouts  27.8 us (6%)
  matrix products  23.7 us (6%)
  between operations  14.9 us (3%)
    reduce_scatter x1, waiting for transfers between devices, per_device(): lax.psum_scatter(grad_parts[0], DP, scatter_dimension=1, tiled=True)  97.1 us
    all_gather x1, waiting for transfers between devices, per_device(): right_full = lax.all_gather(right_basis, DP, axis=1, tiled=True)  56.5 us
    all_gather x1, waiting for transfers between devices, per_device(): lax.all_gather(back_rows, DP, axis=1, tiled=True)  54.2 us
    all_gather x1, waiting for transfers between devices, per_device(): lax.all_gather(new_master.astype(jnp.bfloat16), DP, axis=1, tiled=True)  52.4 us
    unnamed x7, waiting for transfers between devices  46 us
    psum x4, blocking collectives, over_axes(): array = lax.psum(array, axis)  34.8 us
    reduce_scatter x1, waiting for transfers between devices, summed_rows(): parts = lax.psum_scatter(parts, core, scatter_dimension=0, tiled=True)  18.8 us
    optimization_barrier x1, local copies, waits for them, and re-layouts, per_device(): lax.optimization_barrier(raw_term.astype(jnp.bfloat16)).astype(jnp.float32)  11.4 us
  transfers between devices with their start and end apart: 6, of which 6 were waited for; matrix products, arithmetic and copies ran while one was open for 0% of the time, Pallas kernels for 0%

commit v1 on v0

v1 whole, which is shorter than its diff:
```python
import jax
import jax.numpy as jnp
from jax import lax
from jax.experimental import pallas as pl
from jax.experimental.pallas import tpu as pltpu
from jax.sharding import Mesh
from jax.sharding import PartitionSpec as P

D = 4096
STEP = 10
X, Y, CORE, MP = "dp_0", "dp_1", "dp_2", "mp"
DP = (X, Y, CORE)


beta_one = 0.95
beta_two = 0.95
epsilon = 1e-08
norm_epsilon = 1e-06
learning_rate = 0.3
decay_rate = 0.1
bias_one = 1.0 - beta_one**STEP
bias_two = 1.0 - beta_two**STEP


def f32(array):
    return array.astype(jnp.float32)


def low(array):
    return array.astype(jnp.bfloat16)


def shifted(array, axis, step):
    return lax.ppermute(array, axis, [(i, (i + step) % 4) for i in range(4)])


def other_core(array):
    return lax.ppermute(array, CORE, [(0, 1), (1, 0)])


def ring_sum(piece, axis):
    arrived = [shifted(piece(step), axis, step) for step in (1, 3, 2)]
    total = f32(piece(0))
    for term in arrived:
        total = total + f32(term)
    return total


ANYWHERE = pl.BlockSpec(memory_space=pl.ANY)
SCALARS = pl.BlockSpec(memory_space=pltpu.SMEM)
ON_CHIP = pl.BlockSpec(memory_space=pltpu.VMEM)
COST = pl.CostEstimate(flops=4_000_000, bytes_accessed=2_000_000, transcendentals=0)


def kernel_call(body, inputs, outs, waits=(), scratch=(), kinds=None, room=4):
    def whole(place, *refs):
        body(place, *refs[: len(inputs) - 1], *refs[len(inputs) - 1 + len(waits) :])

    return pl.pallas_call(
        whole,
        out_shape=tuple(jax.ShapeDtypeStruct(shape, dtype) for shape, dtype in outs),
        in_specs=[SCALARS] + list(kinds or [ON_CHIP] * (len(inputs) - 1)) + [ANYWHERE] * len(waits),
        out_specs=tuple(ON_CHIP for _ in outs),
        scratch_shapes=list(scratch),
        cost_estimate=COST,
        compiler_params=pltpu.CompilerParams(vmem_limit_bytes=room * 1024 * 1024),
    )(*inputs, *waits)


def in_order(pieces, me):
    shape, dtype = pieces[0].shape, pieces[0].dtype

    def body(place, *refs):
        for step in range(4):
            refs[4][pl.ds(lax.rem(place[0] + 4 - step, 4), 1)] = refs[step][...][None]

    return kernel_call(
        body, [me.reshape(1)] + [pieces[step] for step in range(4)], [((4,) + shape, dtype)]
    )[0]


HALF = (16, 32, 1024)
ORDER = (1, 3, 2, 0)


def pick_terms(parts, where):
    def body(place, parts_ref, *refs):
        x, y, core = place[0], place[1], place[2]
        for n, step in enumerate(ORDER):
            block, row = lax.rem(x + step, 4), lax.rem(y + step, 4)
            for which, side in ((0, 1 - core), (4, core)):
                out = refs[which + n]

                @pl.loop(0, 4)
                def _(k):
                    for j in range(2):
                        out[2 * k + j] = parts_ref[block, j, k, side]
                        out[8 + 2 * k + j] = parts_ref[k, 2 + j, row, side]

    outs = kernel_call(body, [where, parts], [(HALF, jnp.bfloat16)] * 8, room=24)
    return dict(zip(ORDER, outs[:4])), dict(zip(ORDER, outs[4:]))


def gradient_rows(parts, x, y, core):
    theirs, mine = pick_terms(parts, jnp.stack([x, y, core]))
    by_block, by_row = {}, {}
    for step in ORDER:
        mate = other_core(theirs[step])
        ours = mine[step]
        first = low(f32(ours[:8]) + f32(mate[:8])).reshape(4, 2, 32, 1024)
        second = low(f32(ours[8:]) + f32(mate[8:])).reshape(4, 2, 32, 1024)
        by_block[step] = shifted(first, X, step) if step else first
        by_row[step] = shifted(second, Y, step) if step else second
    first = low(sum((f32(by_block[step]) for step in (1, 3, 2)), f32(by_block[0])))
    second = low(sum((f32(by_row[step]) for step in (1, 3, 2)), f32(by_row[0])))
    terms = []
    for array, axis, me in ((first, Y, y), (second, X, x)):
        pieces = {
            step: lax.dynamic_index_in_dim(array, lax.rem(me + step, 4), 0, keepdims=False)
            for step in ORDER
        }
        terms.append([pieces[0]] + [shifted(pieces[step], axis, step) for step in (1, 3, 2)])

    def body(place, *refs):
        out, squares, acc = refs[8:]
        acc[...] = jnp.zeros((32, 1024), jnp.float32)
        for half in range(2):
            ref = refs[4 * half : 4 * half + 4]
            for j in range(2):
                total = f32(ref[0][j]) + f32(ref[1][j]) + f32(ref[2][j]) + f32(ref[3][j])
                out[2 * half + j] = low(total)
                acc[...] += total * total
        all_rows = acc[0:8] + acc[8:16] + acc[16:24] + acc[24:32]
        tile = sum((all_rows[:, k * 128 : k * 128 + 128] for k in range(1, 8)), all_rows[:, :128])
        squares[...] = jnp.sum(tile, axis=0, keepdims=True)

    return kernel_call(
        body,
        [y.reshape(1)] + terms[0] + terms[1],
        [((4, 32, 1024), jnp.bfloat16), ((1, 128), jnp.float32)],
        scratch=[pltpu.VMEM((32, 1024), jnp.float32)],
    )


def everywhere(value):
    rows = jnp.broadcast_to(value, (128, 128))
    return jnp.sum(lax.all_to_all(rows, (X, Y, CORE, MP), 0, 0, tiled=True), axis=0)


def spread(fresh, x, y, core):
    halves = fresh[:2], fresh[2:]
    stacks = []
    for half, axis in zip(halves, (X, Y)):
        arrived = {step: shifted(half, axis, step) for step in (1, 3, 2)}
        stacks.append(jnp.stack([half] + [arrived[step] for step in (1, 2, 3)]))
    mine = [
        [stack] + [shifted(stack, axis, step) for step in (1, 2, 3)]
        for stack, axis in zip(stacks, (Y, X))
    ]
    theirs = [[other_core(piece) for piece in pieces] for pieces in mine]

    def body(place, *refs):
        x, y, core = place[0], place[1], place[2]
        out = refs[16]
        for n, side in ((0, core), (8, 1 - core)):
            for outer in range(4):

                @pl.loop(0, 4)
                def _(inner):
                    for j in range(2):
                        i, row = lax.rem(x + 4 - inner, 4), lax.rem(y + 4 - outer, 4)
                        out[i, j, row, side] = refs[n + outer][inner, j]
                        i, row = lax.rem(x + 4 - outer, 4), lax.rem(y + 4 - inner, 4)
                        out[i, 2 + j, row, side] = refs[n + 4 + outer][inner, j]

    return kernel_call(
        body,
        [jnp.stack([x, y, core])] + mine[0] + mine[1] + theirs[0] + theirs[1],
        [((4, 4, 4, 2, 32, 1024), jnp.bfloat16)],
        room=24,
    )[0]


def cut_for(arrays, x, waits, dtype):
    many = len(arrays)

    def body(place, *refs):
        for step in range(4):
            block = lax.rem(place[0] + step, 4)
            for n in range(many):
                refs[many + step][n] = refs[n][pl.ds(block, 1)][0].astype(dtype)

    return kernel_call(
        body, [x.reshape(1)] + list(arrays), [((many, 32, 1024), dtype)] * 4, waits
    )


def moved(pieces, x):
    arrived = {step: shifted(pieces[step], X, step) for step in (1, 3, 2)}
    arrived[0] = pieces[0]
    return in_order(arrived, x)


def whole_step(grad_parts, master, first_moment, second_moment, left_basis, right_basis):
    x, y, core = (lax.axis_index(axis) for axis in DP)
    grad_low, squares = gradient_rows(grad_parts.reshape(4, 4, 4, 2, 32, 1024), x, y, core)
    grad_low = grad_low.reshape(128, 1024)
    bases = moved(cut_for([right_basis, left_basis], x, (), jnp.bfloat16), x)
    right = lax.all_gather(bases[:, 0], (Y, CORE), axis=1, tiled=True).reshape(1024, 1024)
    left = bases[:, 1].reshape(128, 4, 8, 32).swapaxes(1, 2).reshape(128, 1024)
    moments = moved(cut_for([first_moment, second_moment], x, (), jnp.bfloat16), x)
    squares_sum = jnp.sum(everywhere(squares))
    clip_scale = jnp.minimum(1.0, 2.0 * D / jnp.sqrt(squares_sum + norm_epsilon))
    turned = low(jnp.dot(grad_low, right, preferred_element_type=jnp.float32))
    terms = low(
        lax.dot_general(left, turned, (((0,), (0,)), ((), ())), preferred_element_type=jnp.float32)
    ).reshape(4, 2, 128, 1024)
    mate = other_core(lax.dynamic_index_in_dim(terms, 1 - core, 1, keepdims=False))
    own = lax.dynamic_index_in_dim(terms, core, 1, keepdims=False)

    def chip(step):
        at = lax.rem(y + step, 4)
        return low(
            f32(lax.dynamic_index_in_dim(own, at, 0, keepdims=False))
            + f32(lax.dynamic_index_in_dim(mate, at, 0, keepdims=False))
        )

    rotated = ring_sum(chip, Y)
    clipped = clip_scale * rotated
    first_here = beta_one * f32(moments[:, 0].reshape(128, 1024)) + (1.0 - beta_one) * clipped
    second_here = (
        beta_two * f32(moments[:, 1].reshape(128, 1024)) + (1.0 - beta_two) * clipped * clipped
    )
    direction = low(
        first_here / bias_one / (jnp.sqrt(second_here / bias_two) + epsilon)
    )
    back = low(
        lax.dot_general(direction, right, (((1,), (1,)), ((), ())), preferred_element_type=jnp.float32)
    )
    column = {step: shifted(back, Y, step) for step in (1, 3, 2)}
    column[0] = back
    update = jnp.zeros((128, 1024), jnp.float32)
    for step in (0, 1, 3, 2):
        mate = other_core(column[step])
        source = lax.rem(y + 4 - step, 4)
        for side, rows in ((core, column[step]), (1 - core, mate)):
            part = lax.dynamic_slice(left, (0, source * 256 + side * 128), (128, 128))
            update = update + jnp.dot(part, rows, preferred_element_type=jnp.float32)
    owned = moved(cut_for([low(rotated).reshape(4, 32, 1024)], x, (back,), jnp.bfloat16), x)
    owned = clip_scale * f32(owned[:, 0])
    new_first = beta_one * first_moment + (1.0 - beta_one) * owned
    new_second = beta_two * second_moment + (1.0 - beta_two) * owned * owned
    kept = moved(cut_for([master], x, (back,), jnp.float32), x).reshape(128, 1024)
    fresh = low(kept * (1.0 - learning_rate * decay_rate) - learning_rate * update)
    weights = spread(fresh.reshape(4, 32, 1024), x, y, core).reshape(4, 1024, 1024)
    rows = moved(cut_for([low(update).reshape(4, 32, 1024)], x, (fresh,), jnp.bfloat16), x)
    new_master = master * (1.0 - learning_rate * decay_rate) - learning_rate * f32(rows[:, 0])
    return (weights, new_master, new_first, new_second)


def solution(mesh):
    finer = Mesh(mesh.devices.reshape(4, 4, 2, mesh.shape["mp"]), (X, Y, CORE, MP))
    row_split = P(None, DP, MP)
    return jax.shard_map(
        whole_step,
        mesh=finer,
        in_specs=(P(DP, None, None, MP),) + (row_split,) * 5,
        out_specs=(P(None, None, MP),) + (row_split,) * 3,
        check_vma=False,
    )
```

time: 429 us -> 240 us (0.56)
  waiting for transfers between devices: 325 us -> 90.7 us
  starting transfers between devices: 0.24 us -> 96.3 us
  blocking collectives: 34.8 us -> 0 us
  matrix products: 23.7 us -> 5.57 us
  local copies, waits for them, and re-layouts: 27.8 us -> 11 us
  other arithmetic: 1.88 us -> 13.9 us
  Pallas kernels: 0 us -> 6.51 us
    all_gather x3 -> x1, waiting for transfers between devices: 163 us -> 0.02 us  [whole_step(): lax.all_gather(bases[:, 0], (Y, CORE), axis=1, tiled=True)]
    reduce_scatter x2 -> x0, waiting for transfers between devices: 116 us -> none  [the longest x1 97.1 us: per_device(): lax.psum_scatter(grad_parts[0], DP, scatter_dimension=1, tiled=True)]
    ppermute x0 -> x62, starting transfers between devices: none -> 89.1 us  [the longest x45 59.7 us: shifted(): return lax.ppermute(array, axis, [(i, (i + step) % 4) for i in range(4)])]
    ppermute x0 -> x62, waiting for transfers between devices: none -> 81.1 us  [the longest x45 79.1 us: shifted(): return lax.ppermute(array, axis, [(i, (i + step) % 4) for i in range(4)])]
    unnamed x7 -> x1, waiting for transfers between devices: 46 us -> 0.02 us
    psum x4 -> x0, blocking collectives: 34.8 us -> none  [over_axes(): array = lax.psum(array, axis)]
    dot_general x3 -> x10, matrix products: 23.7 us -> 5.57 us  [the longest x1 2.7 us: whole_step(): lax.dot_general(left, turned, (((0,), (0,)), ((), ())), preferred_element...]
    optimization_barrier x1 -> x0, local copies, waits for them, and re-layouts: 11.4 us -> none  [per_device(): lax.optimization_barrier(raw_term.astype(jnp.bfloat16)).astype(jnp.float32)]
  transfers between devices with their start and end apart: 6 -> 64, of which waited for: 6 -> 21; matrix products, arithmetic and copies ran while one was open for 0% -> 7% of each run, Pallas kernels for 0% -> 1%
where the time goes in v1:
time: 240 us; the launch traced here: 239 us
  starting transfers between devices  96.3 us (40%)
  waiting for transfers between devices  90.7 us (38%)
  between operations  15.2 us (6%)
  other arithmetic  13.9 us (6%)
  local copies, waits for them, and re-layouts  11 us (5%)
  Pallas kernels  6.51 us (3%)
  matrix products  5.57 us (2%)
    ppermute x45, waiting for transfers between devices, shifted(): return lax.ppermute(array, axis, [(i, (i + step) % 4) for i in range(4)])  79.1 us
    ppermute x45, starting transfers between devices, shifted(): return lax.ppermute(array, axis, [(i, (i + step) % 4) for i in range(4)])  59.7 us
    ppermute x17, starting transfers between devices, other_core(): return lax.ppermute(array, CORE, [(0, 1), (1, 0)])  29.4 us
    convert_element_type x8, other arithmetic, low(): return array.astype(jnp.bfloat16)  10.9 us
    all_to_all x1, waiting for transfers between devices, everywhere(): lax.all_to_all(rows, (X, Y, CORE, MP), 0, 0, tiled=True)  9.58 us
    all_to_all x1, starting transfers between devices, everywhere(): lax.all_to_all(rows, (X, Y, CORE, MP), 0, 0, tiled=True)  7.09 us
    pallas_call x13, Pallas kernels, kernel_call(): pl.pallas_call(whole, out_shape=tuple((jax.ShapeDtypeStruct(shape, dtype)...  6.51 us
    unnamed x18, local copies, waits for them, and re-layouts  5.82 us
  transfers between devices with their start and end apart: 64, of which 21 were waited for; matrix products, arithmetic and copies ran while one was open for 7% of the time, Pallas kernels for 1%

profile of v1, /device:TPU:1, one launch (start us, length us, event | category | flops | bytes accessed | tf_op | source)
XLA Modules:
  0.0 239.1 jit_solution(7225362484974829360)
XLA Ops:
  15.4 4.1 %collective-permute-done.20.refs_2_ = bf16[2,32,1024]{2,1,0:T(8,128)(2,1)S(1)} collective-permute-done((bf16[2,32,1024]{2,1,0:T(8,128)(2,1)S(1)}, bf16[2,32,1024]{2,1,0:T(8,128)(2,1)S(1)}, u32[]{:S(2)}, u32[]{:S(2)}) %collective-permute-start.20) | collective-permute-done | bytes 131104 | tf_op jit(solution)/shard_map/ppermute | solution.py:34
  20.3 3.4 %copy-done = bf16[1,4,1024,1024]{3,2,1,0:T(8,128)(2,1)S(1)} copy-done((bf16[1,4,1024,1024]{3,2,1,0:T(8,128)(2,1)S(1)}, bf16[1,4,1024,1024]{3,2,1,0:T(8,128)(2,1)}, u32[]{:S(2)}) %copy-start) | copy-done | bytes 8388632
  39.5 5.3 %collective-permute-done.5 = bf16[4,2,32,1024]{3,2,1,0:T(8,128)(2,1)} collective-permute-done((bf16[4,2,32,1024]{3,2,1,0:T(8,128)(2,1)}, bf16[4,2,32,1024]{3,2,1,0:T(8,128)(2,1)}, u32[]{:S(2)}, u32[]{:S(2)}) %collective-permute-start.5) | collective-permute-done | bytes 524320 | tf_op jit(solution)/shard_map/ppermute | solution.py:34
  44.8 2.9 %collective-permute-start.15 = (bf16[4,2,32,1024]{3,2,1,0:T(8,128)(2,1)}, bf16[4,2,32,1024]{3,2,1,0:T(8,128)(2,1)S(1)}, u32[]{:S(2)}, u32[]{:S(2)}) collective-permute-start(bf16[4,2,32,1024]{3,2,1,0:T(8,128)(2,1)} %bitcast.141), channel_id=1, source_target_pairs={{0,16},{8,24},{16,0},{24,8},{1,17},{9,25},{17,1},{25,9},{2,18},{10... | collective-permute-start | bytes 1572872 | tf_op jit(solution)/shard_map/ppermute | solution.py:34
  48.2 8.3 %collective-permute-done.9 = bf16[4,2,32,1024]{3,2,1,0:T(8,128)(2,1)} collective-permute-done((bf16[4,2,32,1024]{3,2,1,0:T(8,128)(2,1)}, bf16[4,2,32,1024]{3,2,1,0:T(8,128)(2,1)}, u32[]{:S(2)}, u32[]{:S(2)}) %collective-permute-start.9) | collective-permute-done | bytes 524320 | tf_op jit(solution)/shard_map/ppermute | solution.py:34
  58.2 3.1 %collective-permute-start.12 = (bf16[2,32,1024]{2,1,0:T(8,128)(2,1)S(1)}, bf16[2,32,1024]{2,1,0:T(8,128)(2,1)S(1)}, u32[]{:S(2)}, u32[]{:S(2)}) collective-permute-start(bf16[2,32,1024]{2,1,0:T(8,128)(2,1)S(1)} %get-tuple-element.85), channel_id=1, source_target_pairs={{0,16},{8,24},{16,0},{24,8},{1,17},{9,25},{17,1},{25,9},{2,18},{10... | collective-permute-start | bytes 393224 | tf_op jit(solution)/shard_map/ppermute | solution.py:34
  62.8 4.8 %collective-permute-done.15 = bf16[4,2,32,1024]{3,2,1,0:T(8,128)(2,1)S(1)} collective-permute-done((bf16[4,2,32,1024]{3,2,1,0:T(8,128)(2,1)}, bf16[4,2,32,1024]{3,2,1,0:T(8,128)(2,1)S(1)}, u32[]{:S(2)}, u32[]{:S(2)}) %collective-permute-start.15) | collective-permute-done | bytes 524320 | tf_op jit(solution)/shard_map/ppermute | solution.py:34
  68.0 2.8 %collective-permute-start.18 = (bf16[2,32,1024]{2,1,0:T(8,128)(2,1)S(1)}, bf16[2,32,1024]{2,1,0:T(8,128)(2,1)S(1)}, u32[]{:S(2)}, u32[]{:S(2)}) collective-permute-start(bf16[2,32,1024]{2,1,0:T(8,128)(2,1)S(1)} %get-tuple-element.81), channel_id=1, source_target_pairs={{0,64},{32,96},{64,0},{96,32},{1,65},{33,97},{65,1},{97,33},{2,66}... | collective-permute-start | bytes 393224 | tf_op jit(solution)/shard_map/ppermute | solution.py:34
  77.2 2.7 %convolution_convert_fusion = bf16[1024,1024]{1,0:T(8,128)(2,1)S(1)} fusion(bf16[128,1024]{0,1:T(8,128)(2,1)} %bitcast.128, bf16[128,1024]{1,0:T(8,128)(2,1)S(1)} %bitcast.119, bf16[1024,1024]{1,0:T(8,128)(2,1)} %bitcast.122), kind=kOutput, calls=%fused_computation | convolution fusion | flops 538050560 | bytes 4718592 | tf_op jit(solution)/shard_map/dot_general | solution.py:216
  81.6 3.0 %collective-permute-start.22 = (bf16[4,128,1024]{2,1,0:T(8,128)(2,1)}, bf16[4,128,1024]{2,1,0:T(8,128)(2,1)}, u32[]{:S(2)}, u32[]{:S(2)}) collective-permute-start(bf16[4,128,1024]{2,1,0:T(8,128)(2,1)} %dynamic-slice_bitcast_fusion), channel_id=1, source_target_pairs={{0,4},{4,0},{1,5},{5,1},{2,6},{6,2},{3,7},{7,3},{8,12},{12,8},{9,1... | collective-permute-start | bytes 3145736 | tf_op jit(solution)/shard_map/ppermute | solution.py:38
  90.6 4.3 %collective-permute-start.25 = (bf16[128,1024]{1,0:T(8,128)(2,1)}, bf16[128,1024]{1,0:T(8,128)(2,1)}, u32[]{:S(2)}, u32[]{:S(2)}) collective-permute-start(bf16[128,1024]{1,0:T(8,128)(2,1)} %get-tuple-element.67), channel_id=1, source_target_pairs={{0,16},{8,24},{16,0},{24,8},{1,17},{9,25},{17,1},{25,9},{2,18},{10... | collective-permute-start | bytes 786440 | tf_op jit(solution)/shard_map/ppermute | solution.py:34
  98.3 7.1 %all-to-all-start = ((f32[128,1,128]{2,1,0:T(1,128)}), f32[128,1,128]{2,1,0:T(1,128)S(1)}, u32[]{:S(2)}, u32[]{:S(2)}) async-start(f32[128,1,128]{2,1,0:T(1,128)} %broadcast_in_dim.2), calls=%async_computation | async-start | bytes 131072 | tf_op jit(solution)/shard_map/all_to_all | solution.py:147
  105.5 9.6 %all-to-all-done = f32[128,1,128]{2,1,0:T(1,128)S(1)} async-done(((f32[128,1,128]{2,1,0:T(1,128)}), f32[128,1,128]{2,1,0:T(1,128)S(1)}, u32[]{:S(2)}, u32[]{:S(2)}) %all-to-all-start) | async-done | bytes 65568 | tf_op jit(solution)/shard_map/all_to_all | solution.py:147
  127.8 2.7 %collective-permute-start.29 = (bf16[128,1024]{1,0:T(8,128)(2,1)S(1)}, bf16[128,1024]{1,0:T(8,128)(2,1)S(1)}, u32[]{:S(2)}, u32[]{:S(2)}) collective-permute-start(bf16[128,1024]{1,0:T(8,128)(2,1)S(1)} %convolution_convert_fusion.1.refs_1_), channel_id=1, source_target_pairs={{0,4},{4,0},{1,5},{5,1},{2,6},{6,2},{3,7},{7,3},{8,12},{12,8},{9,1... | collective-permute-start | bytes 786440 | tf_op jit(solution)/shard_map/ppermute | solution.py:38
  139.9 3.4 %collective-permute-start.60 = (bf16[1,32,1024]{2,1,0:T(8,128)(2,1)S(1)}, bf16[1,32,1024]{2,1,0:T(8,128)(2,1)S(1)}, u32[]{:S(2)}, u32[]{:S(2)}) collective-permute-start(bf16[1,32,1024]{2,1,0:T(8,128)(2,1)S(1)} %get-tuple-element.62), channel_id=1, source_target_pairs={{0,64},{32,96},{64,0},{96,32},{1,65},{33,97},{65,1},{97,33},{2,66}... | collective-permute-start | bytes 196616 | tf_op jit(solution)/shard_map/ppermute | solution.py:34
  144.9 2.9 %collective-permute-done.42 = bf16[2,32,1024]{2,1,0:T(8,128)(2,1)S(1)} collective-permute-done((bf16[2,32,1024]{2,1,0:T(8,128)(2,1)S(1)}, bf16[2,32,1024]{2,1,0:T(8,128)(2,1)S(1)}, u32[]{:S(2)}, u32[]{:S(2)}) %collective-permute-start.42) | collective-permute-done | bytes 131104 | tf_op jit(solution)/shard_map/ppermute | solution.py:34
  156.5 22.3 %collective-permute-done.38 = bf16[2,32,1024]{2,1,0:T(8,128)(2,1)S(1)} collective-permute-done((bf16[2,32,1024]{2,1,0:T(8,128)(2,1)S(1)}, bf16[2,32,1024]{2,1,0:T(8,128)(2,1)S(1)}, u32[]{:S(2)}, u32[]{:S(2)}) %collective-permute-start.38) | collective-permute-done | bytes 131104 | tf_op jit(solution)/shard_map/ppermute | solution.py:34
  179.9 4.5 %collective-permute-done.37 = bf16[2,32,1024]{2,1,0:T(8,128)(2,1)S(1)} collective-permute-done((bf16[2,32,1024]{2,1,0:T(8,128)(2,1)S(1)}, bf16[2,32,1024]{2,1,0:T(8,128)(2,1)S(1)}, u32[]{:S(2)}, u32[]{:S(2)}) %collective-permute-start.37) | collective-permute-done | bytes 131104 | tf_op jit(solution)/shard_map/ppermute | solution.py:34
  185.7 4.2 %collective-permute-done.36 = bf16[2,32,1024]{2,1,0:T(8,128)(2,1)S(1)} collective-permute-done((bf16[2,32,1024]{2,1,0:T(8,128)(2,1)S(1)}, bf16[2,32,1024]{2,1,0:T(8,128)(2,1)S(1)}, u32[]{:S(2)}, u32[]{:S(2)}) %collective-permute-start.36) | collective-permute-done | bytes 131104 | tf_op jit(solution)/shard_map/ppermute | solution.py:34
  192.9 3.7 %collective-permute-start.48 = (bf16[4,2,32,1024]{3,2,1,0:T(8,128)(2,1)S(1)}, bf16[4,2,32,1024]{3,2,1,0:T(8,128)(2,1)S(1)}, u32[]{:S(2)}, u32[]{:S(2)}) collective-permute-start(bf16[4,2,32,1024]{3,2,1,0:T(8,128)(2,1)S(1)} %pad_maximum_fusion.refs_0_), channel_id=1, source_target_pairs={{0,4},{4,0},{1,5},{5,1},{2,6},{6,2},{3,7},{7,3},{8,12},{12,8},{9,1... | collective-permute-start | bytes 1572872 | tf_op jit(solution)/shard_map/ppermute | solution.py:38
  199.7 10.4 %collective-permute-done.41.refs_3_ = bf16[4,2,32,1024]{3,2,1,0:T(8,128)(2,1)S(1)} collective-permute-done((bf16[4,2,32,1024]{3,2,1,0:T(8,128)(2,1)S(1)}, bf16[4,2,32,1024]{3,2,1,0:T(8,128)(2,1)S(1)}, u32[]{:S(2)}, u32[]{:S(2)}) %collective-permute-start.41) | collective-permute-done | bytes 524320 | tf_op jit(solution)/shard_map/ppermute | solution.py:34
  210.1 11.6 %collective-permute-start.53 = (bf16[4,2,32,1024]{3,2,1,0:T(8,128)(2,1)S(1)}, bf16[4,2,32,1024]{3,2,1,0:T(8,128)(2,1)S(1)}, u32[]{:S(2)}, u32[]{:S(2)}) collective-permute-start(bf16[4,2,32,1024]{3,2,1,0:T(8,128)(2,1)S(1)} %collective-permute-done.45.refs_5_), channel_id=1, source_target_pairs={{0,4},{4,0},{1,5},{5,1},{2,6},{6,2},{3,7},{7,3},{8,12},{12,8},{9,1... | collective-permute-start | bytes 1572872 | tf_op jit(solution)/shard_map/ppermute | solution.py:38
  221.7 2.7 %collective-permute-done.39.refs_1_ = bf16[4,2,32,1024]{3,2,1,0:T(8,128)(2,1)S(1)} collective-permute-done((bf16[4,2,32,1024]{3,2,1,0:T(8,128)(2,1)S(1)}, bf16[4,2,32,1024]{3,2,1,0:T(8,128)(2,1)S(1)}, u32[]{:S(2)}, u32[]{:S(2)}) %collective-permute-start.39) | collective-permute-done | bytes 524320 | tf_op jit(solution)/shard_map/ppermute | solution.py:34
  227.5 4.8 %shard_map.101 = bf16[4,4,4,2,32,1024]{5,4,3,2,1,0:T(8,128)(2,1)} custom-call(s32[3]{0:T(128)S(1)} %pad_add_fusion.place, bf16[4,2,32,1024]{3,2,1,0:T(8,128)(2,1)S(1)} %pad_maximum_fusion.refs_0_, bf16[4,2,32,1024]{3,2,1,0:T(8,128)(2,1)S(1)} %collective-permute-done.39.refs_1_, bf16[4,2,32,1024]{3,2,1,0:T(8,128)(2,1)S(1)} %collective-permute-done.40.refs_2_, ...), custom_call_target="tpu_custom_call" | custom-call | flops 4000000 | bytes 2000000 | tf_op jit(solution)/shard_map/pallas_call | solution.py:59
  (170 shorter events, 89.4 us)
Async XLA Ops:
  7.2 70.1 %all-gather.3.cloned.1.call-start = ((), (), s32[]{:S(2)}) async-start(), calls=%async_computation.1 | async-start | bytes 2359296 | tf_op jit(solution)/shard_map/all_gather | solution.py:209
  30.2 14.6 %collective-permute-start.5 = (bf16[4,2,32,1024]{3,2,1,0:T(8,128)(2,1)}, bf16[4,2,32,1024]{3,2,1,0:T(8,128)(2,1)}, u32[]{:S(2)}, u32[]{:S(2)}) collective-permute-start(bf16[4,2,32,1024]{3,2,1,0:T(8,128)(2,1)} %bitcast.6), channel_id=1, source_target_pairs={{0,32},{32,64},{64,96},{96,0},{1,33},{33,65},{65,97},{97,1},{2,34}... | collective-permute-start | bytes 1572872 | tf_op jit(solution)/shard_map/ppermute | solution.py:34
  32.5 15.6 %collective-permute-start.7 = (bf16[4,2,32,1024]{3,2,1,0:T(8,128)(2,1)}, bf16[4,2,32,1024]{3,2,1,0:T(8,128)(2,1)}, u32[]{:S(2)}, u32[]{:S(2)}) collective-permute-start(bf16[4,2,32,1024]{3,2,1,0:T(8,128)(2,1)} %bitcast.7), channel_id=1, source_target_pairs={{0,96},{32,0},{64,32},{96,64},{1,97},{33,1},{65,33},{97,65},{2,98}... | collective-permute-start | bytes 1572872 | tf_op jit(solution)/shard_map/ppermute | solution.py:34
  35.6 20.8 %collective-permute-start.9 = (bf16[4,2,32,1024]{3,2,1,0:T(8,128)(2,1)}, bf16[4,2,32,1024]{3,2,1,0:T(8,128)(2,1)}, u32[]{:S(2)}, u32[]{:S(2)}) collective-permute-start(bf16[4,2,32,1024]{3,2,1,0:T(8,128)(2,1)} %bitcast.8), channel_id=1, source_target_pairs={{0,64},{32,96},{64,0},{96,32},{1,65},{33,97},{65,1},{97,33},{2,66}... | collective-permute-start | bytes 1572872 | tf_op jit(solution)/shard_map/ppermute | solution.py:34
  36.8 25.3 %collective-permute-start.13 = (bf16[4,2,32,1024]{3,2,1,0:T(8,128)(2,1)}, bf16[4,2,32,1024]{3,2,1,0:T(8,128)(2,1)S(1)}, u32[]{:S(2)}, u32[]{:S(2)}) collective-permute-start(bf16[4,2,32,1024]{3,2,1,0:T(8,128)(2,1)} %bitcast.139), channel_id=1, source_target_pairs={{0,8},{8,16},{16,24},{24,0},{1,9},{9,17},{17,25},{25,1},{2,10},{10... | collective-permute-start | bytes 1572872 | tf_op jit(solution)/shard_map/ppermute | solution.py:34
  38.1 24.7 %collective-permute-start.14 = (bf16[4,2,32,1024]{3,2,1,0:T(8,128)(2,1)}, bf16[4,2,32,1024]{3,2,1,0:T(8,128)(2,1)S(1)}, u32[]{:S(2)}, u32[]{:S(2)}) collective-permute-start(bf16[4,2,32,1024]{3,2,1,0:T(8,128)(2,1)} %bitcast.140), channel_id=1, source_target_pairs={{0,24},{8,0},{16,8},{24,16},{1,25},{9,1},{17,9},{25,17},{2,26},{10... | collective-permute-start | bytes 1572872 | tf_op jit(solution)/shard_map/ppermute | solution.py:34
  44.8 22.7 %collective-permute-start.15 = (bf16[4,2,32,1024]{3,2,1,0:T(8,128)(2,1)}, bf16[4,2,32,1024]{3,2,1,0:T(8,128)(2,1)S(1)}, u32[]{:S(2)}, u32[]{:S(2)}) collective-permute-start(bf16[4,2,32,1024]{3,2,1,0:T(8,128)(2,1)} %bitcast.141), channel_id=1, source_target_pairs={{0,16},{8,24},{16,0},{24,8},{1,17},{9,25},{17,1},{25,9},{2,18},{10... | collective-permute-start | bytes 1572872 | tf_op jit(solution)/shard_map/ppermute | solution.py:34
  58.2 13.4 %collective-permute-start.12 = (bf16[2,32,1024]{2,1,0:T(8,128)(2,1)S(1)}, bf16[2,32,1024]{2,1,0:T(8,128)(2,1)S(1)}, u32[]{:S(2)}, u32[]{:S(2)}) collective-permute-start(bf16[2,32,1024]{2,1,0:T(8,128)(2,1)S(1)} %get-tuple-element.85), channel_id=1, source_target_pairs={{0,16},{8,24},{16,0},{24,8},{1,17},{9,25},{17,1},{25,9},{2,18},{10... | collective-permute-start | bytes 393224 | tf_op jit(solution)/shard_map/ppermute | solution.py:34
  61.3 13.5 %collective-permute-start.11 = (bf16[2,32,1024]{2,1,0:T(8,128)(2,1)S(1)}, bf16[2,32,1024]{2,1,0:T(8,128)(2,1)S(1)}, u32[]{:S(2)}, u32[]{:S(2)}) collective-permute-start(bf16[2,32,1024]{2,1,0:T(8,128)(2,1)S(1)} %get-tuple-element.86), channel_id=1, source_target_pairs={{0,24},{8,0},{16,8},{24,16},{1,25},{9,1},{17,9},{25,17},{2,26},{10... | collective-permute-start | bytes 393224 | tf_op jit(solution)/shard_map/ppermute | solution.py:34
  90.2 26.2 %collective-permute-start.23 = (bf16[128,1024]{1,0:T(8,128)(2,1)}, bf16[128,1024]{1,0:T(8,128)(2,1)}, u32[]{:S(2)}, u32[]{:S(2)}) collective-permute-start(bf16[128,1024]{1,0:T(8,128)(2,1)} %get-tuple-element.66), channel_id=1, source_target_pairs={{0,8},{8,16},{16,24},{24,0},{1,9},{9,17},{17,25},{25,1},{2,10},{10... | collective-permute-start | bytes 786440 | tf_op jit(solution)/shard_map/ppermute | solution.py:34
  90.6 25.8 %collective-permute-start.25 = (bf16[128,1024]{1,0:T(8,128)(2,1)}, bf16[128,1024]{1,0:T(8,128)(2,1)}, u32[]{:S(2)}, u32[]{:S(2)}) collective-permute-start(bf16[128,1024]{1,0:T(8,128)(2,1)} %get-tuple-element.67), channel_id=1, source_target_pairs={{0,16},{8,24},{16,0},{24,8},{1,17},{9,25},{17,1},{25,9},{2,18},{10... | collective-permute-start | bytes 786440 | tf_op jit(solution)/shard_map/ppermute | solution.py:34
  94.9 21.5 %collective-permute-start.24 = (bf16[128,1024]{1,0:T(8,128)(2,1)}, bf16[128,1024]{1,0:T(8,128)(2,1)}, u32[]{:S(2)}, u32[]{:S(2)}) collective-permute-start(bf16[128,1024]{1,0:T(8,128)(2,1)} %get-tuple-element.68), channel_id=1, source_target_pairs={{0,24},{8,0},{16,8},{24,16},{1,25},{9,1},{17,9},{25,17},{2,26},{10... | collective-permute-start | bytes 786440 | tf_op jit(solution)/shard_map/ppermute | solution.py:34
  98.3 16.8 %all-to-all-start = ((f32[128,1,128]{2,1,0:T(1,128)}), f32[128,1,128]{2,1,0:T(1,128)S(1)}, u32[]{:S(2)}, u32[]{:S(2)}) async-start(f32[128,1,128]{2,1,0:T(1,128)} %broadcast_in_dim.2), calls=%async_computation | async-start | bytes 131072 | tf_op jit(solution)/shard_map/all_to_all | solution.py:147
  149.7 47.0 %collective-permute-start.52 = (bf16[4,2,32,1024]{3,2,1,0:T(8,128)(2,1)S(1)}, bf16[4,2,32,1024]{3,2,1,0:T(8,128)(2,1)S(1)}, u32[]{:S(2)}, u32[]{:S(2)}) collective-permute-start(bf16[4,2,32,1024]{3,2,1,0:T(8,128)(2,1)S(1)} %pad_maximum_fusion.1.refs_4_), channel_id=1, source_target_pairs={{0,4},{4,0},{1,5},{5,1},{2,6},{6,2},{3,7},{7,3},{8,12},{12,8},{9,1... | collective-permute-start | bytes 1572872 | tf_op jit(solution)/shard_map/ppermute | solution.py:38
  151.2 47.2 %collective-permute-start.47 = (bf16[4,2,32,1024]{3,2,1,0:T(8,128)(2,1)S(1)}, bf16[4,2,32,1024]{3,2,1,0:T(8,128)(2,1)S(1)}, u32[]{:S(2)}, u32[]{:S(2)}) collective-permute-start(bf16[4,2,32,1024]{3,2,1,0:T(8,128)(2,1)S(1)} %pad_maximum_fusion.1.refs_4_), channel_id=1, source_target_pairs={{0,96},{32,0},{64,32},{96,64},{1,97},{33,1},{65,33},{97,65},{2,98}... | collective-permute-start | bytes 1572872 | tf_op jit(solution)/shard_map/ppermute | solution.py:34
  152.0 46.3 %collective-permute-start.46 = (bf16[4,2,32,1024]{3,2,1,0:T(8,128)(2,1)S(1)}, bf16[4,2,32,1024]{3,2,1,0:T(8,128)(2,1)S(1)}, u32[]{:S(2)}, u32[]{:S(2)}) collective-permute-start(bf16[4,2,32,1024]{3,2,1,0:T(8,128)(2,1)S(1)} %pad_maximum_fusion.1.refs_4_), channel_id=1, source_target_pairs={{0,64},{32,96},{64,0},{96,32},{1,65},{33,97},{65,1},{97,33},{2,66}... | collective-permute-start | bytes 1572872 | tf_op jit(solution)/shard_map/ppermute | solution.py:34
  153.8 45.2 %collective-permute-start.45 = (bf16[4,2,32,1024]{3,2,1,0:T(8,128)(2,1)S(1)}, bf16[4,2,32,1024]{3,2,1,0:T(8,128)(2,1)S(1)}, u32[]{:S(2)}, u32[]{:S(2)}) collective-permute-start(bf16[4,2,32,1024]{3,2,1,0:T(8,128)(2,1)S(1)} %pad_maximum_fusion.1.refs_4_), channel_id=1, source_target_pairs={{0,32},{32,64},{64,96},{96,0},{1,33},{33,65},{65,97},{97,1},{2,34}... | collective-permute-start | bytes 1572872 | tf_op jit(solution)/shard_map/ppermute | solution.py:34
  153.8 25.0 %collective-permute-start.38 = (bf16[2,32,1024]{2,1,0:T(8,128)(2,1)S(1)}, bf16[2,32,1024]{2,1,0:T(8,128)(2,1)S(1)}, u32[]{:S(2)}, u32[]{:S(2)}) collective-permute-start(bf16[2,32,1024]{2,1,0:T(8,128)(2,1)S(1)} %bitcast.142), channel_id=1, source_target_pairs={{0,96},{32,0},{64,32},{96,64},{1,97},{33,1},{65,33},{97,65},{2,98}... | collective-permute-start | bytes 393224 | tf_op jit(solution)/shard_map/ppermute | solution.py:34
  196.6 13.5 %collective-permute-start.41 = (bf16[4,2,32,1024]{3,2,1,0:T(8,128)(2,1)S(1)}, bf16[4,2,32,1024]{3,2,1,0:T(8,128)(2,1)S(1)}, u32[]{:S(2)}, u32[]{:S(2)}) collective-permute-start(bf16[4,2,32,1024]{3,2,1,0:T(8,128)(2,1)S(1)} %pad_maximum_fusion.refs_0_), channel_id=1, source_target_pairs={{0,24},{8,0},{16,8},{24,16},{1,25},{9,1},{17,9},{25,17},{2,26},{10... | collective-permute-start | bytes 1572872 | tf_op jit(solution)/shard_map/ppermute | solution.py:34
  198.3 23.4 %collective-permute-start.40 = (bf16[4,2,32,1024]{3,2,1,0:T(8,128)(2,1)S(1)}, bf16[4,2,32,1024]{3,2,1,0:T(8,128)(2,1)S(1)}, u32[]{:S(2)}, u32[]{:S(2)}) collective-permute-start(bf16[4,2,32,1024]{3,2,1,0:T(8,128)(2,1)S(1)} %pad_maximum_fusion.refs_0_), channel_id=1, source_target_pairs={{0,16},{8,24},{16,0},{24,8},{1,17},{9,25},{17,1},{25,9},{2,18},{10... | collective-permute-start | bytes 1572872 | tf_op jit(solution)/shard_map/ppermute | solution.py:34
  198.4 26.1 %collective-permute-start.39 = (bf16[4,2,32,1024]{3,2,1,0:T(8,128)(2,1)S(1)}, bf16[4,2,32,1024]{3,2,1,0:T(8,128)(2,1)S(1)}, u32[]{:S(2)}, u32[]{:S(2)}) collective-permute-start(bf16[4,2,32,1024]{3,2,1,0:T(8,128)(2,1)S(1)} %pad_maximum_fusion.refs_0_), channel_id=1, source_target_pairs={{0,8},{8,16},{16,24},{24,0},{1,9},{9,17},{17,25},{25,1},{2,10},{10... | collective-permute-start | bytes 1572872 | tf_op jit(solution)/shard_map/ppermute | solution.py:34
  199.0 26.2 %collective-permute-start.55 = (bf16[4,2,32,1024]{3,2,1,0:T(8,128)(2,1)S(1)}, bf16[4,2,32,1024]{3,2,1,0:T(8,128)(2,1)S(1)}, u32[]{:S(2)}, u32[]{:S(2)}) collective-permute-start(bf16[4,2,32,1024]{3,2,1,0:T(8,128)(2,1)S(1)} %collective-permute-done.47.refs_7_), channel_id=1, source_target_pairs={{0,4},{4,0},{1,5},{5,1},{2,6},{6,2},{3,7},{7,3},{8,12},{12,8},{9,1... | collective-permute-start | bytes 1572872 | tf_op jit(solution)/shard_map/ppermute | solution.py:38
  199.6 27.6 %collective-permute-start.54 = (bf16[4,2,32,1024]{3,2,1,0:T(8,128)(2,1)S(1)}, bf16[4,2,32,1024]{3,2,1,0:T(8,128)(2,1)S(1)}, u32[]{:S(2)}, u32[]{:S(2)}) collective-permute-start(bf16[4,2,32,1024]{3,2,1,0:T(8,128)(2,1)S(1)} %collective-permute-done.46.refs_6_), channel_id=1, source_target_pairs={{0,4},{4,0},{1,5},{5,1},{2,6},{6,2},{3,7},{7,3},{8,12},{12,8},{9,1... | collective-permute-start | bytes 1572872 | tf_op jit(solution)/shard_map/ppermute | solution.py:38
  210.1 17.1 %collective-permute-start.53 = (bf16[4,2,32,1024]{3,2,1,0:T(8,128)(2,1)S(1)}, bf16[4,2,32,1024]{3,2,1,0:T(8,128)(2,1)S(1)}, u32[]{:S(2)}, u32[]{:S(2)}) collective-permute-start(bf16[4,2,32,1024]{3,2,1,0:T(8,128)(2,1)S(1)} %collective-permute-done.45.refs_5_), channel_id=1, source_target_pairs={{0,4},{4,0},{1,5},{5,1},{2,6},{6,2},{3,7},{7,3},{8,12},{12,8},{9,1... | collective-permute-start | bytes 1572872 | tf_op jit(solution)/shard_map/ppermute | solution.py:38
  (49 other events, 315.8 us)
Sparse Core Ops, SparseCore 0:
  20.4 31.6 all-gather.2
